TPU v7x, 256 devices: a whole 4x4x8 slice. The times are simulated.
256 devices in a mesh: fsdp: 32 (over y_lo, z, core), tp: 8 (over x, y_hi).
Axes of the slice: x: 4, y: 4 (y_hi: 2, y_lo: 2; y = y_hi * 2 + y_lo), z: 8, core: 2. Of those that a mesh axis runs over, the one named last changes fastest.
Arguments:
- hidden: bfloat16 [64, 5120], P(None, 'fsdp'), may hold values from -20 to 20
- query_weight: bfloat16 [5120, 5120], P(None, ('tp', 'fsdp')), may hold values from -0.078125 to 0.078125
- key_weight: bfloat16 [5120, 1024], P(None, ('tp', 'fsdp')), may hold values from -0.078125 to 0.078125
- value_weight: bfloat16 [5120, 1024], P(None, ('tp', 'fsdp')), may hold values from -0.078125 to 0.078125
- output_weight: bfloat16 [5120, 5120], P(('tp', 'fsdp')), may hold values from -0.078125 to 0.078125
- gate_weight: bfloat16 [5120, 27648], P(None, ('tp', 'fsdp')), may hold values from -0.078125 to 0.078125
- up_weight: bfloat16 [5120, 27648], P(None, ('tp', 'fsdp')), may hold values from -0.078125 to 0.078125
- down_weight: bfloat16 [27648, 5120], P(('tp', 'fsdp')), may hold values from -0.0390625 to 0.0390625
- history: float32 [7, 1024], replicated, may hold values from 0.0001 to 1, as said below
- slot: int32 [1], replicated, may hold values from 0 to 1023
- lengths: int32 [64], P('fsdp'), may hold values from 512 to 4096, as said below
- key_cache: bfloat16 [64, 4096, 1024], P('fsdp', None, 'tp'), may hold values from -1000 to 1000
- value_cache: bfloat16 [64, 4096, 1024], P('fsdp', None, 'tp'), may hold values from -6 to 6
Outputs:
- attention_out: bfloat16 [64, 5120], P('fsdp', 'tp')
- query_rollout: bfloat16 [5120, 5120], P('fsdp', 'tp')
- key_rollout: bfloat16 [5120, 1024], P('fsdp', 'tp')
- value_rollout: bfloat16 [5120, 1024], P('fsdp', 'tp')
- output_rollout: bfloat16 [5120, 5120], P('tp', 'fsdp')
- gate_rollout: bfloat16 [5120, 27648], P('fsdp', 'tp')
- up_rollout: bfloat16 [5120, 27648], P('fsdp', 'tp')
- down_rollout: bfloat16 [27648, 5120], P('tp', 'fsdp')
- new_history: float32 [7, 1024], replicated
Inputs may be any that keep to these rules, and one draw needn't show every extreme that they name: `history`: strictly positive. `lengths`: some sequence has all 4096 slots valid.
All inputs are finite; a program needn't handle non-finite values.
Results may differ from a plain program's by a relative error of at most 0.012.
The roundings to bfloat16 on the way count: a program that leaves them out, or rounds other values in their place, can miss the bound.
Values may be sent and summed in bfloat16 or wider, within the bound.
A program may use at most 64 MiB of HBM per device.

v0:
```python
import math

import jax
import jax.numpy as jnp
from jax import lax
from jax.sharding import Mesh
from jax.sharding import PartitionSpec as P

D = 5120
HEADS = 40
KV_HEADS = 8
HEAD_DIM = 128
FSDP = ("fsdp_0", "fsdp_1", "fsdp_2")
FSDP_TP = ("fsdp_0", "fsdp_1", "fsdp_2", "tp_0", "tp_1")
TP_FSDP = ("tp_0", "tp_1", "fsdp_0", "fsdp_1", "fsdp_2")
TP = ("tp_0", "tp_1")


target_peak = 4.0
norm_eps = 1e-06
rope_theta = 1000000.0


def one_axis_at_a_time(x, axes):
    for axis in axes:
        x = lax.pmax(x, axis)
    return x


def split_up(x, dim, size):
    before, after = (x.shape[:dim], x.shape[dim + 1 :])
    return jnp.moveaxis(x.reshape(*before, size, -1, *after), dim, 0)


def sum_at_owner(x, axis, dim):
    size = lax.axis_size(axis)
    pieces = lax.all_to_all(split_up(x, dim, size), axis, 0, 0, tiled=True)
    return jnp.sum(pieces, axis=0)


def side_by_side(arrays, axis, dim, along):
    widths = [math.prod(a.shape[along:]) for a in arrays]
    both = jnp.concatenate(
        [a.reshape(*a.shape[:along], w) for a, w in zip(arrays, widths)], axis=along
    )
    result = sum_at_owner(both, axis, dim)
    pieces = jnp.split(result, [sum(widths[:k]) for k in range(1, len(widths))], axis=along)
    return tuple(
        (b.reshape(*result.shape[:along], *a.shape[along:]) for a, b in zip(arrays, pieces))
    )


def largest(tensor):
    return jnp.max(jnp.abs(tensor.astype(jnp.float32)))


def scaling(peaks, history, slot):
    marked = lax.broadcasted_iota(jnp.int32, history.shape, 1) == slot[0]
    kept = jnp.max(jnp.where(marked, jnp.zeros_like(history), history), axis=1)
    return (target_peak / jnp.maximum(peaks, kept), jnp.where(marked, peaks[:, None], history))


def quantize(tensor, factor):
    return (tensor.astype(jnp.float32) * factor).astype(jnp.bfloat16)


def rotate(vectors, positions):
    half_dim = vectors.shape[-1] // 2
    ladder = jnp.arange(half_dim, dtype=jnp.float32)
    spread = rope_theta ** (-2.0 * ladder / vectors.shape[-1])
    angle = positions.astype(jnp.float32)[:, None] * spread[None, :]
    cosine = jnp.cos(angle)[:, None, :]
    sine = jnp.sin(angle)[:, None, :]
    first = vectors[..., :half_dim]
    second = vectors[..., half_dim:]
    return jnp.concatenate(
        [first * cosine - second * sine, second * cosine + first * sine], axis=-1
    )


def regroup(query_part, key_part, value_part, output_part, gate_part, up_part, down_part):
    columns = (
        lax.all_to_all(query_part, FSDP, split_axis=0, concat_axis=1, tiled=True),
        lax.all_to_all(key_part, FSDP, split_axis=0, concat_axis=1, tiled=True),
        lax.all_to_all(value_part, FSDP, split_axis=0, concat_axis=1, tiled=True),
        lax.all_to_all(gate_part, FSDP, split_axis=0, concat_axis=1, tiled=True),
        lax.all_to_all(up_part, FSDP, split_axis=0, concat_axis=1, tiled=True),
    )
    rowwise = (
        lax.all_to_all(output_part, FSDP, split_axis=1, concat_axis=0, tiled=True),
        lax.all_to_all(down_part, FSDP, split_axis=1, concat_axis=0, tiled=True),
    )
    return (columns[0], columns[1], columns[2], rowwise[0], columns[3], columns[4], rowwise[1])


def attend(query, key_new, value_new, key_cache, value_cache, lengths):
    count_seq = query.shape[0]
    kv_count = query.shape[1]
    head_dim = query.shape[3]
    cache_len = key_cache.shape[1]
    keys = key_cache.reshape(count_seq, cache_len, kv_count, head_dim)
    values = value_cache.reshape(count_seq, cache_len, kv_count, head_dim)
    scale = head_dim ** (-0.5)
    scores = jnp.einsum("bkgd,bjkd->bkgj", query, keys, preferred_element_type=jnp.float32) * scale
    own = (
        jnp.sum(query.astype(jnp.float32) * key_new.astype(jnp.float32)[:, :, None, :], axis=-1)
        * scale
    )
    valid = (lax.broadcasted_iota(jnp.int32, (count_seq, cache_len), 1) < lengths[:, None])[
        :, None, None, :
    ]
    top = jnp.maximum(jnp.max(jnp.where(valid, scores, -1e30), axis=-1), own)
    weights = jnp.where(valid, jnp.exp(scores - top[..., None]), 0.0)
    own_weight = jnp.exp(own - top)
    total = jnp.sum(weights, axis=-1) + own_weight
    probs = (weights / total[..., None]).astype(jnp.bfloat16)
    own_prob = (own_weight / total).astype(jnp.bfloat16)
    mixed = jnp.einsum("bkgj,bjkd->bkgd", probs, values, preferred_element_type=jnp.float32)
    mixed = (
        mixed
        + own_prob.astype(jnp.float32)[..., None] * value_new.astype(jnp.float32)[:, :, None, :]
    )
    return mixed.astype(jnp.bfloat16).reshape(count_seq, -1)


def per_device(
    hidden,
    query_weight,
    key_weight,
    value_weight,
    output_weight,
    gate_weight,
    up_weight,
    down_weight,
    history,
    slot,
    lengths,
    key_cache,
    value_cache,
):
    trainer = (
        query_weight,
        key_weight,
        value_weight,
        output_weight,
        gate_weight,
        up_weight,
        down_weight,
    )
    peaks = one_axis_at_a_time(jnp.stack([largest(tensor) for tensor in trainer]), FSDP_TP)
    factors, new_history = scaling(peaks, history, slot)
    arrived = regroup(
        query_weight, key_weight, value_weight, output_weight, gate_weight, up_weight, down_weight
    )
    rollout = tuple((quantize(arrived[number], factors[number]) for number in range(7)))
    (
        query_rollout,
        key_rollout,
        value_rollout,
        output_rollout,
        gate_rollout,
        up_rollout,
        down_rollout,
    ) = rollout
    widened = hidden.astype(jnp.float32)
    squares = jnp.sum(widened * widened, axis=1)
    joined = jnp.concatenate([query_rollout, key_rollout, value_rollout], axis=1)
    partial_value = jnp.dot(hidden, joined, preferred_element_type=jnp.float32)
    summed, total_sq = side_by_side((partial_value, squares), FSDP, 0, 1)
    inv_rms = lax.rsqrt(total_sq / D + norm_eps)[:, None]
    width_q = query_rollout.shape[1]
    width_k = key_rollout.shape[1]
    query = summed[:, :width_q] * inv_rms / factors[0]
    key_new = summed[:, width_q : width_q + width_k] * inv_rms / factors[1]
    value_new = summed[:, width_q + width_k :] * inv_rms / factors[2]
    count_seq = summed.shape[0]
    query = rotate(query.reshape(count_seq, -1, HEAD_DIM), lengths).astype(jnp.bfloat16)
    query = query.reshape(count_seq, -1, HEADS // KV_HEADS, HEAD_DIM)
    key_new = rotate(key_new.reshape(count_seq, -1, HEAD_DIM), lengths).astype(jnp.bfloat16)
    value_new = value_new.reshape(count_seq, -1, HEAD_DIM).astype(jnp.bfloat16)
    attention_out = attend(query, key_new, value_new, key_cache, value_cache, lengths)
    return (
        attention_out,
        query_rollout,
        key_rollout,
        value_rollout,
        output_rollout,
        gate_rollout,
        up_rollout,
        down_rollout,
        new_history,
    )


def solution(mesh):
    finer = Mesh(
        mesh.devices.reshape(2, 8, 2, 4, 2), ("fsdp_0", "fsdp_1", "fsdp_2", "tp_0", "tp_1")
    )
    in_specs = (
        P(None, FSDP),
        P(None, TP_FSDP),
        P(None, TP_FSDP),
        P(None, TP_FSDP),
        P(TP_FSDP, None),
        P(None, TP_FSDP),
        P(None, TP_FSDP),
        P(TP_FSDP, None),
        P(),
        P(),
        P(FSDP),
        P(FSDP, None, TP),
        P(FSDP, None, TP),
    )
    out_specs = (
        P(FSDP, TP),
        P(FSDP, TP),
        P(FSDP, TP),
        P(FSDP, TP),
        P(TP, FSDP),
        P(FSDP, TP),
        P(FSDP, TP),
        P(TP, FSDP),
        P(),
    )
    return jax.shard_map(
        per_device, mesh=finer, in_specs=in_specs, out_specs=out_specs, check_vma=False
    )
```

profile of v0, /device:TPU:1, one launch (start us, length us, event | category | flops | bytes accessed | tf_op | source)
XLA Modules:
  0.0 267.1 jit_solution(6872040948014434948)
XLA Ops:
  12.0 4.6 %stack.31 = f32[7]{0:T(128)S(1)} concatenate(f32[1]{0:T(128)} %bitcast, f32[1]{0:T(128)} %bitcast.1, f32[1]{0:T(128)} %bitcast.2, f32[1]{0:T(128)} %bitcast.3, f32[1]{0:T(128)} %bitcast.4, f32[1]{0:T(128)} %bitcast.5, f32[1]{0:T(128)} %bitcast.6), dimensions={0} | concatenate | bytes 56 | tf_op jit(solution)/shard_map/stack | solution.py:150
  16.7 4.4 %pmax.35 = f32[7]{0:T(128)S(1)} all-reduce(f32[7]{0:T(128)S(1)} %stack.31), channel_id=1, replica_groups=mesh['fsdp_0'=2,'fsdp_1'=8,'fsdp_2'=2,'tp_0'=4,'tp_1'=2] {'fsdp_0'}, use_global_device_ids=true, to_apply=%region_7.0 | all-reduce | flops 7 | bytes 56 | tf_op jit(solution)/shard_map/pmax | solution.py:26
  21.8 11.6 %all-to-all-start.1 = ((bf16[32,160,4]{1,2,0:T(4,128)(2,1)}), bf16[32,160,4]{1,2,0:T(4,128)(2,1)S(1)}, u32[]{:S(2)}, u32[]{:S(2)}) async-start(bf16[32,160,4]{1,2,0:T(4,128)(2,1)} %copy.43), calls=%async_computation.1 | async-start | bytes 131072 | tf_op jit(solution)/shard_map/all_to_all | solution.py:84
  33.5 13.6 %pmax.36 = f32[7]{0:T(128)S(1)} all-reduce(f32[7]{0:T(128)S(1)} %pmax.35), channel_id=1, replica_groups=mesh['fsdp_0'=2,'fsdp_1'=8,'fsdp_2'=2,'tp_0'=4,'tp_1'=2] {'fsdp_1'}, use_global_device_ids=true, to_apply=%region_8.0 | all-reduce | flops 7 | bytes 56 | tf_op jit(solution)/shard_map/pmax | solution.py:26
  47.5 5.9 %pmax.37 = f32[7]{0:T(128)S(1)} all-reduce(f32[7]{0:T(128)S(1)} %pmax.36), channel_id=1, replica_groups=mesh['fsdp_0'=2,'fsdp_1'=8,'fsdp_2'=2,'tp_0'=4,'tp_1'=2] {'fsdp_2'}, use_global_device_ids=true, to_apply=%region_9.0 | all-reduce | flops 7 | bytes 56 | tf_op jit(solution)/shard_map/pmax | solution.py:26
  53.5 8.5 %pmax.38 = f32[7]{0:T(128)S(1)} all-reduce(f32[7]{0:T(128)S(1)} %pmax.37), channel_id=1, replica_groups=mesh['fsdp_0'=2,'fsdp_1'=8,'fsdp_2'=2,'tp_0'=4,'tp_1'=2] {'tp_0'}, use_global_device_ids=true, to_apply=%region_10.0 | all-reduce | flops 7 | bytes 56 | tf_op jit(solution)/shard_map/pmax | solution.py:26
  62.4 5.3 %pmax.39 = f32[7]{0:T(128)S(1)} all-reduce(f32[7]{0:T(128)S(1)} %pmax.38), channel_id=1, replica_groups=mesh['fsdp_0'=2,'fsdp_1'=8,'fsdp_2'=2,'tp_0'=4,'tp_1'=2] {'tp_1'}, use_global_device_ids=true, to_apply=%region_11.0 | all-reduce | flops 7 | bytes 56 | tf_op jit(solution)/shard_map/pmax | solution.py:26
  72.1 9.2 %all-to-all-start.2 = ((bf16[32,160,4]{1,2,0:T(4,128)(2,1)}), bf16[32,160,4]{1,2,0:T(4,128)(2,1)S(1)}, u32[]{:S(2)}, u32[]{:S(2)}) async-start(bf16[32,160,4]{1,2,0:T(4,128)(2,1)} %copy.44), calls=%async_computation.2 | async-start | bytes 131072 | tf_op jit(solution)/shard_map/all_to_all | solution.py:85
  81.9 7.4 %all-to-all-done.2 = bf16[32,160,4]{1,2,0:T(4,128)(2,1)S(1)} async-done(((bf16[32,160,4]{1,2,0:T(4,128)(2,1)}), bf16[32,160,4]{1,2,0:T(4,128)(2,1)S(1)}, u32[]{:S(2)}, u32[]{:S(2)}) %all-to-all-start.2) | async-done | bytes 40992 | tf_op jit(solution)/shard_map/all_to_all | solution.py:85
  89.3 4.7 %all-to-all-start = ((bf16[32,160,20]{1,2,0:T(8,128)(2,1)}), bf16[32,160,20]{1,2,0:T(8,128)(2,1)S(1)}, u32[]{:S(2)}, u32[]{:S(2)}) async-start(bf16[32,160,20]{1,2,0:T(8,128)(2,1)} %copy.42), calls=%async_computation | async-start | bytes 786432 | tf_op jit(solution)/shard_map/all_to_all | solution.py:83
  95.5 12.7 %all-to-all-done = bf16[32,160,20]{1,2,0:T(8,128)(2,1)S(1)} async-done(((bf16[32,160,20]{1,2,0:T(8,128)(2,1)}), bf16[32,160,20]{1,2,0:T(8,128)(2,1)S(1)}, u32[]{:S(2)}, u32[]{:S(2)}) %all-to-all-start) | async-done | bytes 204832 | tf_op jit(solution)/shard_map/all_to_all | solution.py:83
  108.2 6.2 %all-to-all-start.4 = ((bf16[20,32,160]{2,0,1:T(8,128)(2,1)}), bf16[20,32,160]{2,0,1:T(8,128)(2,1)}, u32[]{:S(2)}, u32[]{:S(2)}) async-start(bf16[20,32,160]{2,0,1:T(8,128)(2,1)} %copy.46), calls=%async_computation.4 | async-start | bytes 786432 | tf_op jit(solution)/shard_map/all_to_all | solution.py:90
  120.0 8.7 %all-to-all-done.4 = bf16[20,32,160]{2,0,1:T(8,128)(2,1)} async-done(((bf16[20,32,160]{2,0,1:T(8,128)(2,1)}), bf16[20,32,160]{2,0,1:T(8,128)(2,1)}, u32[]{:S(2)}, u32[]{:S(2)}) %all-to-all-start.4) | async-done | bytes 204832 | tf_op jit(solution)/shard_map/all_to_all | solution.py:90
  128.7 5.5 %all-to-all-start.3 = ((f32[32,2,897]{2,1,0:T(2,128)}), f32[32,2,897]{2,1,0:T(2,128)S(1)}, u32[]{:S(2)}, u32[]{:S(2)}) async-start(f32[32,2,897]{2,1,0:T(2,128)} %pad_maximum_fusion), calls=%async_computation.3 | async-start | bytes 524288 | tf_op jit(solution)/shard_map/all_to_all | solution.py:37
  135.7 10.4 %all-to-all-done.3 = f32[32,2,897]{2,1,0:T(2,128)S(1)} async-done(((f32[32,2,897]{2,1,0:T(2,128)}), f32[32,2,897]{2,1,0:T(2,128)S(1)}, u32[]{:S(2)}, u32[]{:S(2)}) %all-to-all-start.3) | async-done | bytes 229664 | tf_op jit(solution)/shard_map/all_to_all | solution.py:37
  146.8 5.2 %all-to-all-start.5 = ((bf16[32,160,108]{2,1,0:T(8,128)(2,1)}), bf16[32,160,108]{2,1,0:T(8,128)(2,1)S(1)}, u32[]{:S(2)}, u32[]{:S(2)}) async-start(bf16[32,160,108]{2,1,0:T(8,128)(2,1)} %bitcast.67), calls=%async_computation.5 | async-start | bytes 2621440 | tf_op jit(solution)/shard_map/all_to_all | solution.py:86
  154.5 30.2 %all-to-all-done.5 = bf16[32,160,108]{2,1,0:T(8,128)(2,1)S(1)} async-done(((bf16[32,160,108]{2,1,0:T(8,128)(2,1)}), bf16[32,160,108]{2,1,0:T(8,128)(2,1)S(1)}, u32[]{:S(2)}, u32[]{:S(2)}) %all-to-all-start.5) | async-done | bytes 1105952 | tf_op jit(solution)/shard_map/all_to_all | solution.py:86
  184.7 5.6 %all-to-all-start.6 = ((bf16[32,160,108]{2,1,0:T(8,128)(2,1)}), bf16[32,160,108]{2,1,0:T(8,128)(2,1)}, u32[]{:S(2)}, u32[]{:S(2)}) async-start(bf16[32,160,108]{2,1,0:T(8,128)(2,1)} %bitcast.66), calls=%async_computation.6 | async-start | bytes 2621440 | tf_op jit(solution)/shard_map/all_to_all | solution.py:87
  207.9 15.1 %all-to-all-done.6 = bf16[32,160,108]{2,1,0:T(8,128)(2,1)} async-done(((bf16[32,160,108]{2,1,0:T(8,128)(2,1)}), bf16[32,160,108]{2,1,0:T(8,128)(2,1)}, u32[]{:S(2)}, u32[]{:S(2)}) %all-to-all-start.6) | async-done | bytes 1105952 | tf_op jit(solution)/shard_map/all_to_all | solution.py:87
  223.0 5.7 %all-to-all-start.7 = ((bf16[108,32,160]{0,2,1:T(8,128)(2,1)}), bf16[108,32,160]{0,2,1:T(8,128)(2,1)}, u32[]{:S(2)}, u32[]{:S(2)}) async-start(bf16[108,32,160]{0,2,1:T(8,128)(2,1)} %bitcast.65), calls=%async_computation.7 | async-start | bytes 2621440 | tf_op jit(solution)/shard_map/all_to_all | solution.py:91
  233.3 2.9 %convert_element_type.233 = bf16[160,3456]{1,0:T(8,128)(2,1)} reshape(bf16[160,32,108]{2,1,0:T(8,128)(2,1)S(1)} %copy.48) | data formatting | bytes 2211840 | tf_op jit(solution)/shard_map/convert_element_type | solution.py:64
  238.9 2.9 %convert_element_type.237 = bf16[160,3456]{1,0:T(8,128)(2,1)} reshape(bf16[160,32,108]{2,1,0:T(8,128)(2,1)S(1)} %copy.50) | data formatting | bytes 2211840 | tf_op jit(solution)/shard_map/convert_element_type | solution.py:64
  241.8 19.7 %all-to-all-done.7 = bf16[108,32,160]{0,2,1:T(8,128)(2,1)} async-done(((bf16[108,32,160]{0,2,1:T(8,128)(2,1)}), bf16[108,32,160]{0,2,1:T(8,128)(2,1)}, u32[]{:S(2)}, u32[]{:S(2)}) %all-to-all-start.7) | async-done | bytes 1105952 | tf_op jit(solution)/shard_map/all_to_all | solution.py:91
  264.2 2.9 %convert_element_type.241 = bf16[3456,160]{0,1:T(8,128)(2,1)} reshape(bf16[32,108,160]{1,0,2:T(8,128)(2,1)S(1)} %copy.52) | data formatting | bytes 2211840 | tf_op jit(solution)/shard_map/convert_element_type | solution.py:64
  (111 shorter events, 56.4 us)
Async XLA Ops:
  0.6 228.6 %copy-start = (bf16[2,4096,128]{2,1,0:T(8,128)(2,1)S(1)}, bf16[2,4096,128]{2,1,0:T(8,128)(2,1)}, u32[]{:S(2)}) copy-start(bf16[2,4096,128]{2,1,0:T(8,128)(2,1)} %param.24) | copy-start | bytes 6291460
  0.7 8.9 %copy-start.2 = (bf16[5120,108]{0,1:T(8,128)(2,1)S(1)}, bf16[5120,108]{0,1:T(8,128)(2,1)}, u32[]{:S(2)}) copy-start(bf16[5120,108]{0,1:T(8,128)(2,1)} %param.19) | copy-start | bytes 3317764
  2.5 8.3 %copy-start.3 = (bf16[108,5120]{1,0:T(8,128)(2,1)S(1)}, bf16[108,5120]{1,0:T(8,128)(2,1)}, u32[]{:S(2)}) copy-start(bf16[108,5120]{1,0:T(8,128)(2,1)} %param.20) | copy-start | bytes 3317764
  9.6 7.0 %copy-start.12 = (bf16[5120,4]{0,1:T(4,128)(2,1)S(1)}, bf16[5120,4]{0,1:T(4,128)(2,1)}, u32[]{:S(2)}) copy-start(bf16[5120,4]{0,1:T(4,128)(2,1)} %param.15) | copy-start | bytes 122884
  9.6 37.5 %copy-start.6 = (bf16[5120,20]{0,1:T(8,128)(2,1)S(1)}, bf16[5120,20]{0,1:T(8,128)(2,1)}, u32[]{:S(2)}) copy-start(bf16[5120,20]{0,1:T(8,128)(2,1)} %param.14) | copy-start | bytes 614404
  10.8 42.6 %copy-start.13 = (bf16[5120,4]{0,1:T(4,128)(2,1)S(1)}, bf16[5120,4]{0,1:T(4,128)(2,1)}, u32[]{:S(2)}) copy-start(bf16[5120,4]{0,1:T(4,128)(2,1)} %param.16) | copy-start | bytes 122884
  10.8 51.2 %copy-start.7 = (bf16[20,5120]{1,0:T(8,128)(2,1)S(1)}, bf16[20,5120]{1,0:T(8,128)(2,1)}, u32[]{:S(2)}) copy-start(bf16[20,5120]{1,0:T(8,128)(2,1)} %param.17) | copy-start | bytes 614404
  10.8 57.6 %copy-start.14 = (f32[7,1024]{1,0:T(8,128)S(1)}, f32[7,1024]{1,0:T(8,128)}, u32[]{:S(2)}) copy-start(f32[7,1024]{1,0:T(8,128)} %param.21) | copy-start | bytes 86020
  12.0 58.9 %copy-start.15 = (bf16[64,160]{1,0:T(8,128)(2,1)S(1)}, bf16[64,160]{1,0:T(8,128)(2,1)}, u32[]{:S(2)}) copy-start(bf16[64,160]{1,0:T(8,128)(2,1)} %param.13) | copy-start | bytes 61444
  21.8 50.2 %all-to-all-start.1 = ((bf16[32,160,4]{1,2,0:T(4,128)(2,1)}), bf16[32,160,4]{1,2,0:T(4,128)(2,1)S(1)}, u32[]{:S(2)}, u32[]{:S(2)}) async-start(bf16[32,160,4]{1,2,0:T(4,128)(2,1)} %copy.43), calls=%async_computation.1 | async-start | bytes 131072 | tf_op jit(solution)/shard_map/all_to_all | solution.py:84
  72.1 17.2 %all-to-all-start.2 = ((bf16[32,160,4]{1,2,0:T(4,128)(2,1)}), bf16[32,160,4]{1,2,0:T(4,128)(2,1)S(1)}, u32[]{:S(2)}, u32[]{:S(2)}) async-start(bf16[32,160,4]{1,2,0:T(4,128)(2,1)} %copy.44), calls=%async_computation.2 | async-start | bytes 131072 | tf_op jit(solution)/shard_map/all_to_all | solution.py:85
  89.3 18.9 %all-to-all-start = ((bf16[32,160,20]{1,2,0:T(8,128)(2,1)}), bf16[32,160,20]{1,2,0:T(8,128)(2,1)S(1)}, u32[]{:S(2)}, u32[]{:S(2)}) async-start(bf16[32,160,20]{1,2,0:T(8,128)(2,1)} %copy.42), calls=%async_computation | async-start | bytes 786432 | tf_op jit(solution)/shard_map/all_to_all | solution.py:83
  94.8 21.2 %copy-start.8 = (bf16[160,128]{0,1:T(8,128)(2,1)}, bf16[160,128]{0,1:T(8,128)(2,1)S(1)}, u32[]{:S(2)}) copy-start(bf16[160,128]{0,1:T(8,128)(2,1)S(1)} %convert_element_type.211) | copy-start | bytes 122884
  95.5 20.5 %copy-start.10 = (bf16[160,128]{0,1:T(8,128)(2,1)}, bf16[160,128]{0,1:T(8,128)(2,1)S(1)}, u32[]{:S(2)}) copy-start(bf16[160,128]{0,1:T(8,128)(2,1)S(1)} %convert_element_type.215) | copy-start | bytes 122884
  108.2 20.4 %all-to-all-start.4 = ((bf16[20,32,160]{2,0,1:T(8,128)(2,1)}), bf16[20,32,160]{2,0,1:T(8,128)(2,1)}, u32[]{:S(2)}, u32[]{:S(2)}) async-start(bf16[20,32,160]{2,0,1:T(8,128)(2,1)} %copy.46), calls=%async_computation.4 | async-start | bytes 786432 | tf_op jit(solution)/shard_map/all_to_all | solution.py:90
  116.0 18.2 %copy-start.1 = (bf16[5120,108]{0,1:T(8,128)(2,1)S(1)}, bf16[5120,108]{0,1:T(8,128)(2,1)}, u32[]{:S(2)}) copy-start(bf16[5120,108]{0,1:T(8,128)(2,1)} %param.18) | copy-start | bytes 3317764
  128.7 17.4 %all-to-all-start.3 = ((f32[32,2,897]{2,1,0:T(2,128)}), f32[32,2,897]{2,1,0:T(2,128)S(1)}, u32[]{:S(2)}, u32[]{:S(2)}) async-start(f32[32,2,897]{2,1,0:T(2,128)} %pad_maximum_fusion), calls=%async_computation.3 | async-start | bytes 524288 | tf_op jit(solution)/shard_map/all_to_all | solution.py:37
  146.8 37.9 %all-to-all-start.5 = ((bf16[32,160,108]{2,1,0:T(8,128)(2,1)}), bf16[32,160,108]{2,1,0:T(8,128)(2,1)S(1)}, u32[]{:S(2)}, u32[]{:S(2)}) async-start(bf16[32,160,108]{2,1,0:T(8,128)(2,1)} %bitcast.67), calls=%async_computation.5 | async-start | bytes 2621440 | tf_op jit(solution)/shard_map/all_to_all | solution.py:86
  184.7 38.3 %all-to-all-start.6 = ((bf16[32,160,108]{2,1,0:T(8,128)(2,1)}), bf16[32,160,108]{2,1,0:T(8,128)(2,1)}, u32[]{:S(2)}, u32[]{:S(2)}) async-start(bf16[32,160,108]{2,1,0:T(8,128)(2,1)} %bitcast.66), calls=%async_computation.6 | async-start | bytes 2621440 | tf_op jit(solution)/shard_map/all_to_all | solution.py:87
  190.3 5.8 %copy-start.11 = (bf16[160,128]{0,1:T(8,128)(2,1)S(1)}, bf16[160,128]{0,1:T(8,128)(2,1)}, u32[]{:S(2)}) copy-start(bf16[160,128]{0,1:T(8,128)(2,1)} %copy-done.10) | copy-start | bytes 122884
  223.0 5.7 %copy-start.21 = (f32[64]{0:T(128)S(1)}, f32[64]{0:T(128)}, u32[]{:S(2)}) copy-start(f32[64]{0:T(128)} %copy-done.20) | copy-start | bytes 772
  223.0 6.0 %copy-start.16 = (f32[2,64]{1,0:T(2,128)S(1)}, f32[2,64]{1,0:T(2,128)}, u32[]{:S(2)}) copy-start(f32[2,64]{1,0:T(2,128)} %get-tuple-element.37) | copy-start | bytes 1540
  223.0 6.0 %copy-start.17 = (f32[2,64]{1,0:T(2,128)S(1)}, f32[2,64]{1,0:T(2,128)}, u32[]{:S(2)}) copy-start(f32[2,64]{1,0:T(2,128)} %get-tuple-element.38) | copy-start | bytes 1540
  223.0 38.5 %all-to-all-start.7 = ((bf16[108,32,160]{0,2,1:T(8,128)(2,1)}), bf16[108,32,160]{0,2,1:T(8,128)(2,1)}, u32[]{:S(2)}, u32[]{:S(2)}) async-start(bf16[108,32,160]{0,2,1:T(8,128)(2,1)} %bitcast.65), calls=%async_computation.7 | async-start | bytes 2621440 | tf_op jit(solution)/shard_map/all_to_all | solution.py:91
  (7 other events, 16.8 us)
where the time goes:
time: 269 us; the launch traced here: 267 us
  waiting for transfers between devices  104 us (39%)
  starting transfers between devices  53.7 us (20%)
  local copies, waits for them, and re-layouts  38.5 us (14%)
  blocking collectives  37.7 us (14%)
  other arithmetic  28 us (10%)
  matrix products  3.25 us (1%)
    pmax x5, blocking collectives, one_axis_at_a_time(): x = lax.pmax(x, axis)  37.7 us
    all_to_all x1, waiting for transfers between devices, regroup(): lax.all_to_all(gate_part, FSDP, split_axis=0, concat_axis=1, tiled=True)  30.2 us
    all_to_all x1, waiting for transfers between devices, regroup(): lax.all_to_all(down_part, FSDP, split_axis=1, concat_axis=0, tiled=True)  19.7 us
    all_to_all x1, waiting for transfers between devices, regroup(): lax.all_to_all(up_part, FSDP, split_axis=0, concat_axis=1, tiled=True)  15.1 us
    unnamed x54, local copies, waits for them, and re-layouts  14.6 us
    convert_element_type x10, local copies, waits for them, and re-layouts, quantize(): return (tensor.astype(jnp.float32) * factor).astype(jnp.bfloat16)  13 us
    all_to_all x1, waiting for transfers between devices, regroup(): lax.all_to_all(query_part, FSDP, split_axis=0, concat_axis=1, tiled=True)  12.7 us
    all_to_all x1, starting transfers between devices, regroup(): lax.all_to_all(key_part, FSDP, split_axis=0, concat_axis=1, tiled=True)  11.6 us
  transfers between devices with their start and end apart: 8, of which 7 were waited for; matrix products, arithmetic and copies ran while one was open for 16% of the time, Pallas kernels for 0%

commit v1 on v0

v1 whole, which is shorter than its diff:
```python
import functools
import math

import jax
import jax.numpy as jnp
import numpy as np
from jax import lax
from jax.experimental import pallas as pl
from jax.experimental.pallas import tpu as pltpu
from jax.sharding import PartitionSpec as P

D = 5120
HEADS = 40
KV_HEADS = 8
HEAD_DIM = 128
GROUP = HEADS // KV_HEADS
CACHE = 4096
HIST = 1024
N = 32
TP = 8
ROWS = D // N
WIDE = 27648 // (N * TP)
SLIM = D // (N * TP)
TINY = KV_HEADS * HEAD_DIM // (N * TP)
LANES = 128
HEAD_COLS = LANES - SLIM - 2 * TINY
REST = WIDE - HEAD_COLS
CHUNK = 512

target_peak = 4.0
norm_eps = 1e-06
rope_theta = 1000000.0

F32 = jnp.float32
BF16 = jnp.bfloat16
MESH = pl.DeviceIdType.MESH


def offset(i):
    k = i // 4
    return (i // 2) % 2, ((k + 1) // 2) * (2 * (k % 2) - 1), i % 2


def kernel(
    hid, wq_h, wk_h, wv_h, wo_h, wg_h, wu_h, wd_h, hist, slot, lens, kc_h, vc_h, spread,
    att_o, q_o, k_o, v_o, o_o, g_o, u_o, d_o, nh_o,
    wq, wk, wv, wo, wg, wu, wd, kc, vc, sent, got, fac,
    pk_s, pk_r, pt_s, pt_r, part, one_r, two_s, two_r,
    load_sem, send_sem, recv_sem, pks_sem, pkr_sem, pts_sem, ptr_sem,
    ones_sem, oner_sem, twos_sem, twor_sem,
):
    me = lax.axis_index("fsdp")
    tp = lax.axis_index("tp")
    my_y, my_z, my_c = me // 16, (me // 2) % 8, me % 2

    def target(i):
        dy, dz, dc = offset(i)
        return ((my_y + dy) % 2) * 16 + ((my_z + dz + 8) % 8) * 2 + (my_c + dc) % 2

    def source(i):
        dy, dz, dc = offset(i)
        return ((my_y + dy) % 2) * 16 + ((my_z - dz + 8) % 8) * 2 + (my_c + dc) % 2

    barrier = pltpu.get_barrier_semaphore()

    def greet(i, _):
        pl.semaphore_signal(barrier, 1, device_id={"fsdp": target(i)}, device_id_type=MESH)
        return 0

    lax.fori_loop(1, N, greet, 0)

    def greet_tp(i, _):
        pl.semaphore_signal(barrier, 1, device_id={"tp": (tp + i) % TP}, device_id_type=MESH)
        return 0

    lax.fori_loop(1, TP, greet_tp, 0)

    loads = [
        pltpu.make_async_copy(src, dst, load_sem.at[n])
        for n, (src, dst) in enumerate(
            [(wg_h, wg), (wq_h, wq), (wk_h, wk), (wv_h, wv), (wu_h, wu), (wd_h, wd), (wo_h, wo), (kc_h, kc), (vc_h, vc)]
        )
    ]
    for load in loads:
        load.start()

    shift = (WIDE * me) % LANES

    def pack(tile, parts):
        def body(c, _):
            cols = pl.ds(pl.multiple_of(c * CHUNK, CHUNK), CHUNK)
            pieces = [ref[lo:hi, cols].astype(F32) for ref, lo, hi in parts]
            rows = sum(hi - lo for _, lo, hi in parts)
            if rows < LANES:
                pieces.append(jnp.zeros((LANES - rows, CHUNK), F32))
            block = jnp.concatenate(pieces, axis=0).T
            sent[tile, cols, :] = pltpu.roll(block, shift, 1).astype(BF16)
            return 0

        lax.fori_loop(0, D // CHUNK, body, 0)

    def block_copy(tile, to, slot_of):
        return pltpu.make_async_remote_copy(
            sent.at[tile, pl.ds(pl.multiple_of(to * ROWS, ROWS), ROWS)],
            got.at[tile, slot_of],
            send_sem.at[tile, to],
            recv_sem.at[tile, slot_of],
            device_id={"fsdp": to},
            device_id_type=MESH,
        )

    def send(tile):
        def body(j, _):
            block_copy(tile, target(N - 1 - j), me).start()
            return 0

        lax.fori_loop(0, N - 1, body, 0)

    for n in range(4):
        loads[n].wait()
    pack(0, [(wg, 0, HEAD_COLS), (wq, 0, SLIM), (wk, 0, TINY), (wv, 0, TINY)])
    for n in range(4, 7):
        loads[n].wait()

    lane = lax.broadcasted_iota(jnp.int32, (1, LANES), 1)
    mine = jnp.zeros((1, LANES), F32)
    for t, ref in enumerate((wq, wk, wv, wo, wg, wu, wd)):
        def body(c, best, ref=ref):
            cols = pl.ds(pl.multiple_of(c * CHUNK, CHUNK), CHUNK)
            return jnp.maximum(best, jnp.max(jnp.abs(ref[:, cols].astype(F32)), axis=0, keepdims=True))

        best = lax.fori_loop(0, D // CHUNK, body, jnp.zeros((1, CHUNK), F32))
        mine = jnp.where(lane == t, jnp.max(best, axis=1, keepdims=True), mine)
    pk_s[...] = mine

    pl.semaphore_wait(barrier, N - 1 + TP - 1)

    def peak_copy(to, slot_of):
        return pltpu.make_async_remote_copy(
            pk_s, pk_r.at[slot_of], pks_sem.at[to], pkr_sem.at[slot_of], device_id={"fsdp": to}, device_id_type=MESH
        )

    def send_peak(j, _):
        peak_copy(target(N - 1 - j), me).start()
        return 0

    lax.fori_loop(0, N - 1, send_peak, 0)
    send(0)
    pack(1, [(wu, 0, WIDE), (wg, HEAD_COLS, WIDE)])
    send(1)

    def wait_peak(j, best):
        src = source(N - 1 - j)
        peak_copy(src, src).wait_recv()
        return jnp.maximum(best, pk_r[src])

    pt_s[...] = lax.fori_loop(0, N - 1, wait_peak, mine)

    def tp_copy(to, slot_of):
        return pltpu.make_async_remote_copy(
            pt_s, pt_r.at[slot_of], pts_sem.at[to], ptr_sem.at[slot_of], device_id={"tp": to}, device_id_type=MESH
        )

    def send_tp(i, _):
        tp_copy((tp + i) % TP, tp).start()
        return 0

    lax.fori_loop(1, TP, send_tp, 0)
    pack(2, [(wd, 0, WIDE), (wo, 0, SLIM)])

    def wait_tp(i, best):
        src = (tp + TP - i) % TP
        tp_copy(src, src).wait_recv()
        return jnp.maximum(best, pt_r[src])

    peaks = lax.fori_loop(1, TP, wait_tp, pt_s[...])

    on_row = lax.broadcasted_iota(jnp.int32, (7, LANES), 0) == lax.broadcasted_iota(jnp.int32, (7, LANES), 1)
    peaks_column = jnp.sum(jnp.where(on_row, peaks, 0.0), axis=1, keepdims=True)
    marked = lax.broadcasted_iota(jnp.int32, (7, HIST), 1) == slot[0]
    past = hist[...]
    kept = jnp.max(jnp.where(marked, 0.0, past), axis=1, keepdims=True)
    nh_o[...] = jnp.where(marked, peaks_column, past)
    fac[0:7, :] = jnp.broadcast_to(target_peak / jnp.maximum(peaks_column, kept), (7, LANES))

    def put(ref, tile, mask, value):
        cols = pl.ds(pl.multiple_of(tile * LANES, LANES), LANES)
        ref[:, cols] = jnp.where(mask, value, ref[:, cols].astype(F32)).astype(BF16)

    def place(ref, first, count, value):
        tiles = ref.shape[1] // LANES
        tile, at = first // LANES, first % LANES
        put(ref, tile, (lane >= at) & (lane < at + count), value)
        if tiles > 1:
            put(ref, tile + 1 - (tile + 1) // tiles, lane < at + count - LANES, value)

    def turn(value, now, then):
        return pltpu.roll(value, (then - now + 4 * LANES) % LANES, 1)

    def process(tile, block, s):
        x = block.astype(F32)
        base = (WIDE * s) % LANES
        if tile == 0:
            place(g_o, WIDE * s, HEAD_COLS, x * fac[4:5, :])
            place(q_o, SLIM * s, SLIM, turn(x * fac[0:1, :], base + HEAD_COLS, (SLIM * s) % LANES))
            place(k_o, TINY * s, TINY, turn(x * fac[1:2, :], base + HEAD_COLS + SLIM, TINY * s))
            place(v_o, TINY * s, TINY, turn(x * fac[2:3, :], base + HEAD_COLS + SLIM + TINY, TINY * s))
        elif tile == 1:
            place(u_o, WIDE * s, WIDE, x * fac[5:6, :])
            place(g_o, WIDE * s + HEAD_COLS, REST, turn(x * fac[4:5, :], base + WIDE, (WIDE * s + HEAD_COLS) % LANES))
        else:
            place(d_o, WIDE * s, WIDE, x * fac[6:7, :])
            place(o_o, SLIM * s, SLIM, turn(x * fac[3:4, :], base + WIDE, (SLIM * s) % LANES))

    def receive(tile):
        process(tile, sent[tile, pl.ds(pl.multiple_of(me * ROWS, ROWS), ROWS), :], me)

        def body(j, _):
            src = source(N - 1 - j)
            block_copy(tile, src, src).wait_recv()
            process(tile, got[tile, src], src)
            return 0

        lax.fori_loop(0, N - 1, body, 0)

    receive(0)

    row = lax.broadcasted_iota(jnp.int32, (64, 64), 0)
    col = lax.broadcasted_iota(jnp.int32, (64, 64), 1)
    owner = (row // 32) * 32 + ((row // 2) % 8) * 4 + ((row // 16) % 2) * 2 + row % 2
    ordered = jnp.dot((owner == col).astype(BF16), hid[...], preferred_element_type=F32)
    hidden = ordered.astype(BF16)
    part[:, 0:640] = jnp.dot(hidden, q_o[...], preferred_element_type=F32)
    part[:, 640:768] = jnp.dot(hidden, k_o[...], preferred_element_type=F32)
    part[:, 768:896] = jnp.dot(hidden, v_o[...], preferred_element_type=F32)
    part[:, 896:1024] = jnp.broadcast_to(jnp.sum(ordered * ordered, axis=1, keepdims=True), (64, LANES))

    group = my_y * 2 + my_c

    def one_copy(k, receiving):
        y, c = (my_y + k // 2) % 2, (my_c + k % 2) % 2
        other = y * 2 + c
        return other, pltpu.make_async_remote_copy(
            part.at[pl.ds(pl.multiple_of(other * 16, 16), 16)],
            one_r.at[other if receiving else group],
            ones_sem.at[other],
            oner_sem.at[other if receiving else group],
            device_id={"fsdp": y * 16 + my_z * 2 + c},
            device_id_type=MESH,
        )

    for k in range(1, 4):
        one_copy(k, False)[1].start()
    total = part[pl.ds(pl.multiple_of(group * 16, 16), 16), :]
    for k in range(1, 4):
        other, copy = one_copy(k, True)
        copy.wait_recv()
        total = total + one_r[other]
    for z in range(8):
        two_s[z] = total[2 * z : 2 * z + 2, :]

    def two_copy(z, slot_of):
        return pltpu.make_async_remote_copy(
            two_s.at[z],
            two_r.at[slot_of],
            twos_sem.at[z],
            twor_sem.at[slot_of],
            device_id={"fsdp": my_y * 16 + z * 2 + my_c},
            device_id_type=MESH,
        )

    def send_two(i, _):
        two_copy((my_z + i) % 8, my_z).start()
        return 0

    lax.fori_loop(1, 8, send_two, 0)
    send(2)
    receive(1)

    def wait_two(i, total):
        src = (my_z + 8 - i) % 8
        two_copy(src, src).wait_recv()
        return total + two_r[src]

    summed = lax.fori_loop(1, 8, wait_two, two_s[my_z])

    inv_rms = lax.rsqrt(summed[:, 896:1024] / D + norm_eps)
    token = lax.broadcasted_iota(jnp.int32, (2, LANES), 0)
    length = jnp.where(token == 0, lens[0], lens[1])
    angle = length.astype(F32) * spread[...]
    half = lax.broadcasted_iota(jnp.int32, (2, LANES), 1) < HEAD_DIM // 2
    cosine = jnp.cos(angle)
    sine = jnp.where(half, -jnp.sin(angle), jnp.sin(angle))

    def rotate(x):
        return x * cosine + pltpu.roll(x, HEAD_DIM // 2, 1) * sine

    heads = [
        rotate(summed[:, h * LANES : (h + 1) * LANES] * inv_rms / fac[0:1, :]).astype(BF16).astype(F32)
        for h in range(GROUP)
    ]
    key_new = rotate(summed[:, 640:768] * inv_rms / fac[1:2, :]).astype(BF16).astype(F32)
    value_new = (summed[:, 768:896] * inv_rms / fac[2:3, :]).astype(BF16).astype(F32)
    loads[7].wait()
    loads[8].wait()
    head_row = lax.broadcasted_iota(jnp.int32, (8, LANES), 0)
    scale = HEAD_DIM ** (-0.5)
    mixes = []
    for b in range(2):
        query = jnp.zeros((8, LANES), F32)
        for h in range(GROUP):
            query = jnp.where(head_row == h, heads[h][b : b + 1, :], query)
        scores = (
            lax.dot_general(query.astype(BF16), kc[b], (((1,), (1,)), ((), ())), preferred_element_type=F32) * scale
        )
        own = jnp.sum(query * key_new[b : b + 1, :], axis=1, keepdims=True) * scale
        valid = lax.broadcasted_iota(jnp.int32, (8, CACHE), 1) < lens[b]
        top = jnp.maximum(jnp.max(jnp.where(valid, scores, -1e30), axis=1, keepdims=True), own)
        weights = jnp.where(valid, jnp.exp(scores - top), 0.0)
        own_weight = jnp.exp(own - top)
        total = jnp.sum(weights, axis=1, keepdims=True) + own_weight
        probs = (weights / total).astype(BF16)
        own_prob = (own_weight / total).astype(BF16).astype(F32)
        mixed = jnp.dot(probs, vc[b], preferred_element_type=F32)
        mixes.append(mixed + own_prob * value_new[b : b + 1, :])
    for h in range(GROUP):
        pair = jnp.where(token == 0, mixes[0][h : h + 1, :], mixes[1][h : h + 1, :])
        att_o[:, h * LANES : (h + 1) * LANES] = pair.astype(BF16)

    receive(2)

    def drain(j, _):
        to = target(N - 1 - j)
        peak_copy(to, me).wait_send()
        for tile in range(3):
            block_copy(tile, to, me).wait_send()
        return 0

    lax.fori_loop(0, N - 1, drain, 0)

    def drain_tp(i, _):
        tp_copy((tp + i) % TP, tp).wait_send()
        return 0

    lax.fori_loop(1, TP, drain_tp, 0)
    for k in range(1, 4):
        one_copy(k, False)[1].wait_send()

    def drain_two(i, _):
        two_copy((my_z + i) % 8, my_z).wait_send()
        return 0

    lax.fori_loop(1, 8, drain_two, 0)


def per_device(
    hidden, query_weight, key_weight, value_weight, output_weight, gate_weight, up_weight, down_weight,
    history, slot, lengths, key_cache, value_cache,
):
    spread = np.float64(rope_theta) ** (-2.0 * (np.arange(HEAD_DIM) % (HEAD_DIM // 2)) / HEAD_DIM)
    spread = jnp.asarray(spread.astype(np.float32)[None, :])
    vmem = pl.BlockSpec(memory_space=pltpu.VMEM)
    smem = pl.BlockSpec(memory_space=pltpu.SMEM)
    hbm = pl.BlockSpec(memory_space=pl.ANY)
    out = [
        ((2, GROUP * HEAD_DIM), BF16),
        ((ROWS, 640), BF16),
        ((ROWS, 128), BF16),
        ((ROWS, 128), BF16),
        ((ROWS, 640), BF16),
        ((ROWS, 3456), BF16),
        ((ROWS, 3456), BF16),
        ((ROWS, 3456), BF16),
        ((7, HIST), F32),
    ]
    dma = pltpu.SemaphoreType.DMA
    results = pl.pallas_call(
        kernel,
        out_shape=[jax.ShapeDtypeStruct(s, t) for s, t in out],
        in_specs=[vmem] + [hbm] * 7 + [vmem, smem, smem, hbm, hbm, vmem],
        out_specs=[vmem] * 9,
        scratch_shapes=[
            pltpu.VMEM((SLIM, D), BF16),
            pltpu.VMEM((TINY, D), BF16),
            pltpu.VMEM((TINY, D), BF16),
            pltpu.VMEM((SLIM, D), BF16),
            pltpu.VMEM((WIDE, D), BF16),
            pltpu.VMEM((WIDE, D), BF16),
            pltpu.VMEM((WIDE, D), BF16),
            pltpu.VMEM((2, CACHE, HEAD_DIM), BF16),
            pltpu.VMEM((2, CACHE, HEAD_DIM), BF16),
            pltpu.VMEM((3, D, LANES), BF16),
            pltpu.VMEM((3, N, ROWS, LANES), BF16),
            pltpu.VMEM((8, LANES), F32),
            pltpu.VMEM((1, LANES), F32),
            pltpu.VMEM((N, 1, LANES), F32),
            pltpu.VMEM((1, LANES), F32),
            pltpu.VMEM((TP, 1, LANES), F32),
            pltpu.VMEM((64, 1024), F32),
            pltpu.VMEM((4, 16, 1024), F32),
            pltpu.VMEM((8, 2, 1024), F32),
            pltpu.VMEM((8, 2, 1024), F32),
            dma((9,)),
            dma((3, N)),
            dma((3, N)),
            dma((N,)),
            dma((N,)),
            dma((TP,)),
            dma((TP,)),
            dma((4,)),
            dma((4,)),
            dma((8,)),
            dma((8,)),
        ],
        compiler_params=pltpu.CompilerParams(
            collective_id=0, has_side_effects=True, vmem_limit_bytes=58 * 2**20
        ),
    )(
        hidden, query_weight.T, key_weight.T, value_weight.T, output_weight, gate_weight.T, up_weight.T, down_weight,
        history, slot, lengths, key_cache, value_cache, spread,
    )
    attention_out, query, key, value, output, gate, up, down, new_history = results
    return attention_out, query, key, value, output.T, gate, up, down.T, new_history


def solution(mesh):
    f, t = "fsdp", "tp"
    in_specs = (
        P(None, f), P(None, (t, f)), P(None, (t, f)), P(None, (t, f)), P((t, f), None), P(None, (t, f)),
        P(None, (t, f)), P((t, f), None), P(), P(), P(f), P(f, None, t), P(f, None, t),
    )
    out_specs = (P(f, t), P(f, t), P(f, t), P(f, t), P(t, f), P(f, t), P(f, t), P(t, f), P())
    return jax.shard_map(per_device, mesh=mesh, in_specs=in_specs, out_specs=out_specs, check_vma=False)
```

time: 269 us -> 123 us (0.46)
  Pallas kernels: 0 us -> 109 us
  waiting for transfers between devices: 104 us -> 0 us
  starting transfers between devices: 53.7 us -> 0 us
  blocking collectives: 37.7 us -> 0 us
  other arithmetic: 28 us -> 0 us
  local copies, waits for them, and re-layouts: 38.5 us -> 13 us
  matrix products: 3.25 us -> 0 us
    pallas_call x0 -> x1, Pallas kernels: none -> 109 us  [per_device(): pl.pallas_call(kernel, out_shape=[jax.ShapeDtypeStruct(s, t) for s, t in...]
    all_to_all x8 -> x0, waiting for transfers between devices: 104 us -> none  [the longest x1 30.2 us: regroup(): lax.all_to_all(gate_part, FSDP, split_axis=0, concat_axis=1, tiled=True)]
    all_to_all x8 -> x0, starting transfers between devices: 53.7 us -> none  [the longest x1 11.6 us: regroup(): lax.all_to_all(key_part, FSDP, split_axis=0, concat_axis=1, tiled=True)]
    pmax x5 -> x0, blocking collectives: 37.7 us -> none  [one_axis_at_a_time(): x = lax.pmax(x, axis)]
    convert_element_type x10 -> x0, local copies, waits for them, and re-layouts: 13 us -> none  [quantize(): return (tensor.astype(jnp.float32) * factor).astype(jnp.bfloat16)]
    reduce_max x7 -> x0, other arithmetic: 11.3 us -> none  [largest(): return jnp.max(jnp.abs(tensor.astype(jnp.float32)))]
    convert_element_type x11 -> x0, other arithmetic: 11.1 us -> none  [the longest x7 9.67 us: quantize(): return (tensor.astype(jnp.float32) * factor).astype(jnp.bfloat16)]
    another operation x1 -> x0, local copies, waits for them, and re-layouts: 4.62 us -> none  [per_device(): jnp.stack([largest(tensor) for tensor in trainer])]
  transfers between devices with their start and end apart: 8 -> 0, of which waited for: 7 -> 0; matrix products, arithmetic and copies ran while one was open for 16% -> 0% of each run, Pallas kernels for 0% -> 0%
where the time goes in v1:
time: 123 us
  Pallas kernels  109 us (89%)
  local copies, waits for them, and re-layouts  13 us (11%)
  between operations  1.31 us (1%)
    pallas_call x1, Pallas kernels, per_device(): pl.pallas_call(kernel, out_shape=[jax.ShapeDtypeStruct(s, t) for s, t in...  109 us
    unnamed x15, local copies, waits for them, and re-layouts  13 us

profile of v1, /device:TPU:1, one launch (start us, length us, event | category | flops | bytes accessed | tf_op | source)
XLA Modules:
  0.0 122.8 jit_solution(17353141419238385369)
XLA Ops:
  1.3 108.5 %shard_map.205 = (bf16[2,640]{1,0:T(2,128)(2,1)}, bf16[160,640]{1,0:T(8,128)(2,1)}, bf16[160,128]{1,0:T(8,128)(2,1)}, bf16[160,128]{1,0:T(8,128)(2,1)}, bf16[160...) custom-call(bf16[64,160]{1,0:T(8,128)(2,1)} %hid.1, ...), custom_call_target="tpu_custom_call" | custom-call | tf_op jit(solution)/shard_map/pallas_call | solution.py:377
  109.8 1.3 %copy.33 = bf16[2,640]{1,0:T(2,128)(2,1)} copy(bf16[2,640]{1,0:T(2,128)(2,1)} %get-tuple-element.36) | data formatting | bytes 5120
  111.1 1.6 %copy.34 = bf16[160,640]{1,0:T(8,128)(2,1)} copy(bf16[160,640]{1,0:T(8,128)(2,1)} %get-tuple-element.37) | data formatting | bytes 409600
  112.7 1.4 %copy.35 = bf16[160,128]{1,0:T(8,128)(2,1)} copy(bf16[160,128]{1,0:T(8,128)(2,1)} %get-tuple-element.38) | data formatting | bytes 81920
  114.1 1.4 %copy.36 = bf16[160,128]{1,0:T(8,128)(2,1)} copy(bf16[160,128]{1,0:T(8,128)(2,1)} %get-tuple-element.39) | data formatting | bytes 81920
  115.5 1.6 %copy.37 = bf16[640,160]{0,1:T(8,128)(2,1)} copy(bf16[640,160]{0,1:T(8,128)(2,1)} %bitcast.11) | data formatting | bytes 409600
  117.1 0.0 copy-start.1
  117.2 2.4 %copy.38 = bf16[160,3456]{1,0:T(8,128)(2,1)} copy(bf16[160,3456]{1,0:T(8,128)(2,1)} %get-tuple-element.41) | data formatting | bytes 2211840
  119.6 0.0 copy-done.1
  119.6 0.0 copy-start
  119.6 1.0 copy.39
  120.5 0.7 copy-done
  121.2 0.0 copy-start.2
  121.2 1.0 copy.40
  122.2 0.0 copy-done.2
  122.2 0.6 copy.41
Async XLA Ops:
  117.1 2.4 %copy-start.1 = (bf16[160,3456]{1,0:T(8,128)(2,1)S(1)}, bf16[160,3456]{1,0:T(8,128)(2,1)}, u32[]{:S(2)}) copy-start(bf16[160,3456]{1,0:T(8,128)(2,1)} %get-tuple-element.42) | copy-start | bytes 3317764
  119.6 1.6 %copy-start = (bf16[160,3456]{1,0:T(8,128)(2,1)S(1)}, bf16[160,3456]{1,0:T(8,128)(2,1)}, u32[]{:S(2)}) copy-start(bf16[160,3456]{1,0:T(8,128)(2,1)} %get-tuple-element.25) | copy-start | bytes 3317764
  121.2 1.0 copy-start.2

commit v2 on v1

--- a/solution.py
+++ b/solution.py
@@ -26,6 +26,7 @@
 HEAD_COLS = LANES - SLIM - 2 * TINY
 REST = WIDE - HEAD_COLS
 CHUNK = 512
+VMEM_LIMIT = 40 * 2**20
 
 target_peak = 4.0
 norm_eps = 1e-06
@@ -42,9 +43,9 @@
 
 
 def kernel(
-    hid, wq_h, wk_h, wv_h, wo_h, wg_h, wu_h, wd_h, hist, slot, lens, kc_h, vc_h, spread,
+    hid_h, wq_h, wk_h, wv_h, wo_h, wg_h, wu_h, wd_h, hist_h, slot, lens_h, kc_h, vc_h, spread_h,
     att_o, q_o, k_o, v_o, o_o, g_o, u_o, d_o, nh_o,
-    wq, wk, wv, wo, wg, wu, wd, kc, vc, sent, got, fac,
+    wq, wk, wv, wo, wg, wu, wd, kc, vc, hid, hist, spread, lens, sent, got, fac,
     pk_s, pk_r, pt_s, pt_r, part, one_r, two_s, two_r,
     load_sem, send_sem, recv_sem, pks_sem, pkr_sem, pts_sem, ptr_sem,
     ones_sem, oner_sem, twos_sem, twor_sem,
@@ -78,7 +79,8 @@
     loads = [
         pltpu.make_async_copy(src, dst, load_sem.at[n])
         for n, (src, dst) in enumerate(
-            [(wg_h, wg), (wq_h, wq), (wk_h, wk), (wv_h, wv), (wu_h, wu), (wd_h, wd), (wo_h, wo), (kc_h, kc), (vc_h, vc)]
+            [(wg_h, wg), (wq_h, wq), (wk_h, wk), (wv_h, wv), (wu_h, wu), (wd_h, wd), (wo_h, wo),
+             (hid_h, hid), (hist_h, hist), (spread_h, spread), (lens_h, lens), (kc_h, kc), (vc_h, vc)]
         )
     ]
     for load in loads:
@@ -175,6 +177,8 @@
 
     peaks = lax.fori_loop(1, TP, wait_tp, pt_s[...])
 
+    for n in range(7, 11):
+        loads[n].wait()
     on_row = lax.broadcasted_iota(jnp.int32, (7, LANES), 0) == lax.broadcasted_iota(jnp.int32, (7, LANES), 1)
     peaks_column = jnp.sum(jnp.where(on_row, peaks, 0.0), axis=1, keepdims=True)
     marked = lax.broadcasted_iota(jnp.int32, (7, HIST), 1) == slot[0]
@@ -301,8 +305,8 @@
     ]
     key_new = rotate(summed[:, 640:768] * inv_rms / fac[1:2, :]).astype(BF16).astype(F32)
     value_new = (summed[:, 768:896] * inv_rms / fac[2:3, :]).astype(BF16).astype(F32)
-    loads[7].wait()
-    loads[8].wait()
+    loads[11].wait()
+    loads[12].wait()
     head_row = lax.broadcasted_iota(jnp.int32, (8, LANES), 0)
     scale = HEAD_DIM ** (-0.5)
     mixes = []
@@ -353,6 +357,15 @@
     lax.fori_loop(1, 8, drain_two, 0)
 
 
+def finish(*refs):
+    count = (len(refs) - 1) // 2
+    copies = [pltpu.make_async_copy(refs[n], refs[count + n], refs[-1].at[n]) for n in range(count)]
+    for copy in copies:
+        copy.start()
+    for copy in copies:
+        copy.wait()
+
+
 def per_device(
     hidden, query_weight, key_weight, value_weight, output_weight, gate_weight, up_weight, down_weight,
     history, slot, lengths, key_cache, value_cache,
@@ -360,8 +373,7 @@
     spread = np.float64(rope_theta) ** (-2.0 * (np.arange(HEAD_DIM) % (HEAD_DIM // 2)) / HEAD_DIM)
     spread = jnp.asarray(spread.astype(np.float32)[None, :])
     vmem = pl.BlockSpec(memory_space=pltpu.VMEM)
-    smem = pl.BlockSpec(memory_space=pltpu.SMEM)
-    hbm = pl.BlockSpec(memory_space=pl.ANY)
+    hbm = pl.BlockSpec(memory_space=pltpu.HBM)
     out = [
         ((2, GROUP * HEAD_DIM), BF16),
         ((ROWS, 640), BF16),
@@ -376,8 +388,8 @@
     dma = pltpu.SemaphoreType.DMA
     results = pl.pallas_call(
         kernel,
-        out_shape=[jax.ShapeDtypeStruct(s, t) for s, t in out],
-        in_specs=[vmem] + [hbm] * 7 + [vmem, smem, smem, hbm, hbm, vmem],
+        out_shape=[pltpu.VMEM(s, t) for s, t in out],
+        in_specs=[hbm] * 9 + [pl.BlockSpec(memory_space=pltpu.SMEM)] + [hbm] * 4,
         out_specs=[vmem] * 9,
         scratch_shapes=[
             pltpu.VMEM((SLIM, D), BF16),
@@ -389,6 +401,10 @@
             pltpu.VMEM((WIDE, D), BF16),
             pltpu.VMEM((2, CACHE, HEAD_DIM), BF16),
             pltpu.VMEM((2, CACHE, HEAD_DIM), BF16),
+            pltpu.VMEM((64, ROWS), BF16),
+            pltpu.VMEM((7, HIST), F32),
+            pltpu.VMEM((1, LANES), F32),
+            pltpu.SMEM((2,), jnp.int32),
             pltpu.VMEM((3, D, LANES), BF16),
             pltpu.VMEM((3, N, ROWS, LANES), BF16),
             pltpu.VMEM((8, LANES), F32),
@@ -400,7 +416,7 @@
             pltpu.VMEM((4, 16, 1024), F32),
             pltpu.VMEM((8, 2, 1024), F32),
             pltpu.VMEM((8, 2, 1024), F32),
-            dma((9,)),
+            dma((13,)),
             dma((3, N)),
             dma((3, N)),
             dma((N,)),
@@ -413,12 +429,25 @@
             dma((8,)),
         ],
         compiler_params=pltpu.CompilerParams(
-            collective_id=0, has_side_effects=True, vmem_limit_bytes=58 * 2**20
+            collective_id=0, has_side_effects=True, vmem_limit_bytes=VMEM_LIMIT
         ),
     )(
-        hidden, query_weight.T, key_weight.T, value_weight.T, output_weight, gate_weight.T, up_weight.T, down_weight,
-        history, slot, lengths, key_cache, value_cache, spread,
+        *(
+            x if x is slot else pltpu.with_memory_space_constraint(x, pltpu.HBM)
+            for x in (
+                hidden, query_weight.T, key_weight.T, value_weight.T, output_weight, gate_weight.T, up_weight.T,
+                down_weight, history, slot, lengths, key_cache, value_cache, spread,
+            )
+        )
     )
+    results = pl.pallas_call(
+        finish,
+        out_shape=[jax.ShapeDtypeStruct(s, t) for s, t in out],
+        in_specs=[vmem] * 9,
+        out_specs=[hbm] * 9,
+        scratch_shapes=[dma((9,))],
+        compiler_params=pltpu.CompilerParams(vmem_limit_bytes=8 * 2**20),
+    )(*results)
     attention_out, query, key, value, output, gate, up, down, new_history = results
     return attention_out, query, key, value, output.T, gate, up, down.T, new_history
 

time: 123 us -> 109 us (0.89)
  local copies, waits for them, and re-layouts: 13 us -> 0 us
    unnamed x15 -> x0, local copies, waits for them, and re-layouts: 13 us -> none
    pallas_call x1 -> x2, Pallas kernels: 109 us -> 108 us  [the longest x1 106 us: per_device(): pl.pallas_call(kernel, out_shape=[pltpu.VMEM(s, t) for s, t in out], in_s...]
where the time goes in v2:
time: 109 us
  Pallas kernels  108 us (99%)
  between operations  1.3 us (1%)
    pallas_call x1, Pallas kernels, per_device(): pl.pallas_call(kernel, out_shape=[pltpu.VMEM(s, t) for s, t in out], in_s...  106 us

profile of v2, /device:TPU:1, one launch (start us, length us, event | category | flops | bytes accessed | tf_op | source)
XLA Modules:
  0.0 109.3 jit_solution(217049287432505109)
XLA Ops:
  1.3 106.0 %shard_map.205 = (bf16[2,640]{1,0:T(2,128)(2,1)S(1)}, bf16[160,640]{1,0:T(8,128)(2,1)S(1)}, bf16[160,128]{1,0:T(8,128)(2,1)S(1)}, bf16[160,128]{1,0:T(8,128)(2,1...) custom-call(bf16[64,160]{1,0:T(8,128)(2,1)} %hid_h.1, ...), custom_call_target="tpu_custom_call" | custom-call | tf_op jit(solution)/shard_map/pallas_call | solution.py:389
  107.3 2.0 %shard_map.206 = (bf16[2,640]{1,0:T(2,128)(2,1)}, bf16[160,640]{1,0:T(8,128)(2,1)}, bf16[160,128]{1,0:T(8,128)(2,1)}, bf16[160,128]{1,0:T(8,128)(2,1)}, bf16[160...) custom-call(bf16[2,640]{1,0:T(2,128)(2,1)S(1)} %get-tuple-element.27, ...), custom_call_target="tpu_custom_call" | custom-call | tf_op jit(solution)/shard_map/pallas_call | solution.py:443

commit v3 on v2

--- a/solution.py
+++ b/solution.py
@@ -38,8 +38,11 @@
 
 
 def offset(i):
-    k = i // 4
-    return (i // 2) % 2, ((k + 1) // 2) * (2 * (k % 2) - 1), i % 2
+    k = lax.div(i, 4) if isinstance(i, jax.Array) else i // 4
+    odd = lax.rem(k, 2) if isinstance(i, jax.Array) else k % 2
+    if isinstance(i, jax.Array):
+        return lax.rem(lax.div(i, 2), 2), lax.rem(lax.div(k + 1, 2) * (2 * odd - 1) + 8, 8), lax.rem(i, 2)
+    return (i // 2) % 2, ((k + 1) // 2 * (2 * odd - 1)) % 8, i % 2
 
 
 def kernel(
@@ -52,29 +55,22 @@
 ):
     me = lax.axis_index("fsdp")
     tp = lax.axis_index("tp")
-    my_y, my_z, my_c = me // 16, (me // 2) % 8, me % 2
-
-    def target(i):
-        dy, dz, dc = offset(i)
-        return ((my_y + dy) % 2) * 16 + ((my_z + dz + 8) % 8) * 2 + (my_c + dc) % 2
+    my_y, my_z, my_c = lax.div(me, 16), lax.rem(lax.div(me, 2), 8), lax.rem(me, 2)
+
+    def device(dy, dz, dc):
+        return lax.rem(my_y + dy, 2) * 16 + lax.rem(my_z + dz, 8) * 2 + lax.rem(my_c + dc, 2)
 
     def source(i):
         dy, dz, dc = offset(i)
-        return ((my_y + dy) % 2) * 16 + ((my_z - dz + 8) % 8) * 2 + (my_c + dc) % 2
+        return device(dy, 8 - dz, dc)
+
+    partners = [device(*offset(i)) for i in range(N - 1, 0, -1)]
 
     barrier = pltpu.get_barrier_semaphore()
-
-    def greet(i, _):
-        pl.semaphore_signal(barrier, 1, device_id={"fsdp": target(i)}, device_id_type=MESH)
-        return 0
-
-    lax.fori_loop(1, N, greet, 0)
-
-    def greet_tp(i, _):
-        pl.semaphore_signal(barrier, 1, device_id={"tp": (tp + i) % TP}, device_id_type=MESH)
-        return 0
-
-    lax.fori_loop(1, TP, greet_tp, 0)
+    for to in partners:
+        pl.semaphore_signal(barrier, 1, device_id={"fsdp": to}, device_id_type=MESH)
+    for i in range(1, TP):
+        pl.semaphore_signal(barrier, 1, device_id={"tp": lax.rem(tp + i, TP)}, device_id_type=MESH)
 
     loads = [
         pltpu.make_async_copy(src, dst, load_sem.at[n])
@@ -86,7 +82,7 @@
     for load in loads:
         load.start()
 
-    shift = (WIDE * me) % LANES
+    shift = lax.rem(WIDE * me, LANES)
 
     def pack(tile, parts):
         def body(c, _):
@@ -101,22 +97,19 @@
 
         lax.fori_loop(0, D // CHUNK, body, 0)
 
-    def block_copy(tile, to, slot_of):
+    def block_copy(tile, to, slot_of, j=0):
         return pltpu.make_async_remote_copy(
             sent.at[tile, pl.ds(pl.multiple_of(to * ROWS, ROWS), ROWS)],
             got.at[tile, slot_of],
-            send_sem.at[tile, to],
+            send_sem.at[tile, j],
             recv_sem.at[tile, slot_of],
             device_id={"fsdp": to},
             device_id_type=MESH,
         )
 
     def send(tile):
-        def body(j, _):
-            block_copy(tile, target(N - 1 - j), me).start()
-            return 0
-
-        lax.fori_loop(0, N - 1, body, 0)
+        for j, to in enumerate(partners):
+            block_copy(tile, to, me, j).start()
 
     for n in range(4):
         loads[n].wait()
@@ -137,16 +130,13 @@
 
     pl.semaphore_wait(barrier, N - 1 + TP - 1)
 
-    def peak_copy(to, slot_of):
+    def peak_copy(to, slot_of, j=0):
         return pltpu.make_async_remote_copy(
-            pk_s, pk_r.at[slot_of], pks_sem.at[to], pkr_sem.at[slot_of], device_id={"fsdp": to}, device_id_type=MESH
-        )
-
-    def send_peak(j, _):
-        peak_copy(target(N - 1 - j), me).start()
-        return 0
-
-    lax.fori_loop(0, N - 1, send_peak, 0)
+            pk_s, pk_r.at[slot_of], pks_sem.at[j], pkr_sem.at[slot_of], device_id={"fsdp": to}, device_id_type=MESH
+        )
+
+    for j, to in enumerate(partners):
+        peak_copy(to, me, j).start()
     send(0)
     pack(1, [(wu, 0, WIDE), (wg, HEAD_COLS, WIDE)])
     send(1)
@@ -158,20 +148,17 @@
 
     pt_s[...] = lax.fori_loop(0, N - 1, wait_peak, mine)
 
-    def tp_copy(to, slot_of):
+    def tp_copy(to, slot_of, i=0):
         return pltpu.make_async_remote_copy(
-            pt_s, pt_r.at[slot_of], pts_sem.at[to], ptr_sem.at[slot_of], device_id={"tp": to}, device_id_type=MESH
-        )
-
-    def send_tp(i, _):
-        tp_copy((tp + i) % TP, tp).start()
-        return 0
-
-    lax.fori_loop(1, TP, send_tp, 0)
+            pt_s, pt_r.at[slot_of], pts_sem.at[i], ptr_sem.at[slot_of], device_id={"tp": to}, device_id_type=MESH
+        )
+
+    for i in range(1, TP):
+        tp_copy(lax.rem(tp + i, TP), tp, i).start()
     pack(2, [(wd, 0, WIDE), (wo, 0, SLIM)])
 
     def wait_tp(i, best):
-        src = (tp + TP - i) % TP
+        src = lax.rem(tp + TP - i, TP)
         tp_copy(src, src).wait_recv()
         return jnp.maximum(best, pt_r[src])
 
@@ -193,28 +180,28 @@
 
     def place(ref, first, count, value):
         tiles = ref.shape[1] // LANES
-        tile, at = first // LANES, first % LANES
+        tile, at = lax.div(first, LANES), lax.rem(first, LANES)
         put(ref, tile, (lane >= at) & (lane < at + count), value)
         if tiles > 1:
-            put(ref, tile + 1 - (tile + 1) // tiles, lane < at + count - LANES, value)
+            put(ref, tile + 1 - lax.div(tile + 1, tiles), lane < at + count - LANES, value)
 
     def turn(value, now, then):
-        return pltpu.roll(value, (then - now + 4 * LANES) % LANES, 1)
+        return pltpu.roll(value, lax.rem(then - now + 4 * LANES, LANES), 1)
 
     def process(tile, block, s):
         x = block.astype(F32)
-        base = (WIDE * s) % LANES
+        base = lax.rem(WIDE * s, LANES)
         if tile == 0:
             place(g_o, WIDE * s, HEAD_COLS, x * fac[4:5, :])
-            place(q_o, SLIM * s, SLIM, turn(x * fac[0:1, :], base + HEAD_COLS, (SLIM * s) % LANES))
+            place(q_o, SLIM * s, SLIM, turn(x * fac[0:1, :], base + HEAD_COLS, lax.rem(SLIM * s, LANES)))
             place(k_o, TINY * s, TINY, turn(x * fac[1:2, :], base + HEAD_COLS + SLIM, TINY * s))
             place(v_o, TINY * s, TINY, turn(x * fac[2:3, :], base + HEAD_COLS + SLIM + TINY, TINY * s))
         elif tile == 1:
             place(u_o, WIDE * s, WIDE, x * fac[5:6, :])
-            place(g_o, WIDE * s + HEAD_COLS, REST, turn(x * fac[4:5, :], base + WIDE, (WIDE * s + HEAD_COLS) % LANES))
+            place(g_o, WIDE * s + HEAD_COLS, REST, turn(x * fac[4:5, :], base + WIDE, lax.rem(WIDE * s + HEAD_COLS, LANES)))
         else:
             place(d_o, WIDE * s, WIDE, x * fac[6:7, :])
-            place(o_o, SLIM * s, SLIM, turn(x * fac[3:4, :], base + WIDE, (SLIM * s) % LANES))
+            place(o_o, SLIM * s, SLIM, turn(x * fac[3:4, :], base + WIDE, lax.rem(SLIM * s, LANES)))
 
     def receive(tile):
         process(tile, sent[tile, pl.ds(pl.multiple_of(me * ROWS, ROWS), ROWS), :], me)
@@ -242,7 +229,7 @@
     group = my_y * 2 + my_c
 
     def one_copy(k, receiving):
-        y, c = (my_y + k // 2) % 2, (my_c + k % 2) % 2
+        y, c = lax.rem(my_y + k // 2, 2), lax.rem(my_c + k % 2, 2)
         other = y * 2 + c
         return other, pltpu.make_async_remote_copy(
             part.at[pl.ds(pl.multiple_of(other * 16, 16), 16)],
@@ -263,26 +250,23 @@
     for z in range(8):
         two_s[z] = total[2 * z : 2 * z + 2, :]
 
-    def two_copy(z, slot_of):
+    def two_copy(z, slot_of, i=0):
         return pltpu.make_async_remote_copy(
             two_s.at[z],
             two_r.at[slot_of],
-            twos_sem.at[z],
+            twos_sem.at[i],
             twor_sem.at[slot_of],
             device_id={"fsdp": my_y * 16 + z * 2 + my_c},
             device_id_type=MESH,
         )
 
-    def send_two(i, _):
-        two_copy((my_z + i) % 8, my_z).start()
-        return 0
-
-    lax.fori_loop(1, 8, send_two, 0)
+    for i in range(1, 8):
+        two_copy(lax.rem(my_z + i, 8), my_z, i).start()
     send(2)
     receive(1)
 
     def wait_two(i, total):
-        src = (my_z + 8 - i) % 8
+        src = lax.rem(my_z + 8 - i, 8)
         two_copy(src, src).wait_recv()
         return total + two_r[src]
 
@@ -331,30 +315,19 @@
         pair = jnp.where(token == 0, mixes[0][h : h + 1, :], mixes[1][h : h + 1, :])
         att_o[:, h * LANES : (h + 1) * LANES] = pair.astype(BF16)
 
-    receive(2)
-
-    def drain(j, _):
-        to = target(N - 1 - j)
-        peak_copy(to, me).wait_send()
-        for tile in range(3):
-            block_copy(tile, to, me).wait_send()
-        return 0
-
-    lax.fori_loop(0, N - 1, drain, 0)
-
-    def drain_tp(i, _):
-        tp_copy((tp + i) % TP, tp).wait_send()
-        return 0
-
-    lax.fori_loop(1, TP, drain_tp, 0)
+    for j, to in enumerate(partners):
+        peak_copy(to, me, j).wait_send()
+        for tile in range(2):
+            block_copy(tile, to, me, j).wait_send()
+    for i in range(1, TP):
+        tp_copy(lax.rem(tp + i, TP), tp, i).wait_send()
     for k in range(1, 4):
         one_copy(k, False)[1].wait_send()
-
-    def drain_two(i, _):
-        two_copy((my_z + i) % 8, my_z).wait_send()
-        return 0
-
-    lax.fori_loop(1, 8, drain_two, 0)
+    for i in range(1, 8):
+        two_copy(lax.rem(my_z + i, 8), my_z, i).wait_send()
+    receive(2)
+    for j, to in enumerate(partners):
+        block_copy(2, to, me, j).wait_send()
 
 
 def finish(*refs):

time: 109 us -> 106 us (0.972)
  Pallas kernels: 108 us -> 104 us
    pallas_call x1, Pallas kernels: 106 us -> 103 us  [per_device(): pl.pallas_call(kernel, out_shape=[pltpu.VMEM(s, t) for s, t in out], in_s...]
where the time goes in v3:
time: 106 us
  Pallas kernels  104 us (98%)
  between operations  1.3 us (1%)
    pallas_call x1, Pallas kernels, per_device(): pl.pallas_call(kernel, out_shape=[pltpu.VMEM(s, t) for s, t in out], in_s...  103 us

profile of v3, /device:TPU:1, one launch (start us, length us, event | category | flops | bytes accessed | tf_op | source)
XLA Modules:
  0.0 105.8 jit_solution(7506767123587839037)
XLA Ops:
  1.3 102.5 %shard_map.205 = (bf16[2,640]{1,0:T(2,128)(2,1)S(1)}, bf16[160,640]{1,0:T(8,128)(2,1)S(1)}, bf16[160,128]{1,0:T(8,128)(2,1)S(1)}, bf16[160,128]{1,0:T(8,128)(2,1...) custom-call(bf16[64,160]{1,0:T(8,128)(2,1)} %hid_h.1, ...), custom_call_target="tpu_custom_call" | custom-call | tf_op jit(solution)/shard_map/pallas_call | solution.py:362
  103.8 2.0 %shard_map.206 = (bf16[2,640]{1,0:T(2,128)(2,1)}, bf16[160,640]{1,0:T(8,128)(2,1)}, bf16[160,128]{1,0:T(8,128)(2,1)}, bf16[160,128]{1,0:T(8,128)(2,1)}, bf16[160...) custom-call(bf16[2,640]{1,0:T(2,128)(2,1)S(1)} %get-tuple-element.27, ...), custom_call_target="tpu_custom_call" | custom-call | tf_op jit(solution)/shard_map/pallas_call | solution.py:416
